TPU v7x, 32 devices: a whole 2x2x4 slice. The times are simulated.
32 devices in a mesh: section: 4 (over y, x), row: 8 (over z, core).
Axes of the slice: x: 2, y: 2, z: 4, core: 2. Of those that a mesh axis runs over, the one named last changes fastest.
Arguments:
- omega: bfloat16 [2048, 8192], P('section', 'row'), may hold values from -0.5 to 0.5
- basis: bfloat16 [8192, 1024], P('row', 'section'), may hold values from -6 to 6
- vectors: bfloat16 [4, 8192], P(None, 'row'), may hold values from -6 to 6
Outputs:
- ortho: float32 [4, 8192], P(None, ('row', 'section'))
- coeffs: float32 [4, 1024], P(None, 'section')
All inputs are finite; a program needn't handle non-finite values.
Results may differ from a plain program's by a relative error of at most 0.0021.
Values may be sent and summed in bfloat16 or wider, within the bound.
A program may use at most 64 MiB of HBM per device.

v0:
```python
import jax
import jax.numpy as jnp
from jax import lax
from jax.sharding import PartitionSpec as P


def from_behind(value, axis, steps):
    count = lax.axis_size(axis)
    initial, last = (max(0, -steps), min(count, count - steps))
    return lax.ppermute(value, axis, [(source, source + steps) for source in range(initial, last)])


def from_root(value, axis, source):
    kept = jnp.where(lax.axis_index(axis) == source, value, 0).astype(value.dtype)
    return lax.psum(kept, axis)


def lower_solve(factor, right):
    return lax.linalg.triangular_solve(factor, right, left_side=True, lower=True, transpose_a=False)


def factor_solve(factor, right):
    half = lower_solve(factor, right)
    return lax.linalg.triangular_solve(factor, half, left_side=True, lower=True, transpose_a=True)


def body(omega, basis, vectors):
    hi = lax.Precision.HIGHEST
    sections = lax.axis_size("section")
    my_section = lax.axis_index("section")
    whole = lax.all_gather(omega, "section", axis=0, tiled=True)
    sketch = lax.psum_scatter(
        jnp.dot(whole, basis, preferred_element_type=jnp.float32),
        "row",
        scatter_dimension=0,
        tiled=True,
    )
    probe_term = lax.dot_general(
        vectors, whole, (((1,), (1,)), ((), ())), preferred_element_type=jnp.float32
    )
    probe = lax.psum_scatter(probe_term, "row", scatter_dimension=1, tiled=True)
    gram = lax.psum(jnp.dot(sketch.T, sketch, precision=hi), "row")
    factor = jnp.linalg.cholesky(gram)

    def project(current):
        inner = jnp.dot(current, sketch, precision=hi)
        inner = lax.psum(inner, "row")
        coef = factor_solve(factor, inner.T).T
        return (coef, current - jnp.dot(coef, sketch.T, precision=hi))

    def advance(step, carry):
        current, kept = carry
        coef, moved = project(current)
        active = my_section == step
        kept = jnp.where(active, coef, kept)
        moved = jnp.where(active, moved, current)
        return (from_behind(moved, "section", 1), kept)

    start_coef = jnp.zeros((vectors.shape[0], basis.shape[1]), jnp.float32)
    probe, kept = lax.fori_loop(0, sections - 1, advance, (probe, start_coef))
    coef, moved = project(probe)
    finished = my_section == sections - 1
    kept = jnp.where(finished, coef, kept)
    final = from_root(moved, "section", sections - 1)
    rounded = kept.astype(jnp.bfloat16)
    own_term = lax.dot_general(
        rounded, basis, (((1,), (1,)), ((), ())), preferred_element_type=jnp.float32
    )
    removed = lax.psum_scatter(own_term, "section", scatter_dimension=1, tiled=True)
    width = removed.shape[1]
    mine = lax.dynamic_slice_in_dim(vectors, my_section * width, width, 1)
    remain = mine.astype(jnp.float32) - removed
    small = lax.psum(jnp.dot(final, final.T, precision=hi), "row")
    lower = jnp.linalg.cholesky(small)
    ortho = lower_solve(lower, remain)
    return (ortho, kept)


def solution(mesh):
    return jax.shard_map(
        body,
        mesh=mesh,
        in_specs=(P("section", "row"), P("row", "section"), P(None, "row")),
        out_specs=(P(None, ("row", "section")), P(None, "section")),
        check_vma=False,
    )
```

profile of v0, /device:TPU:0, one launch (start us, length us, event | category | flops | bytes accessed | tf_op | source)
XLA Modules:
  0.0 442.4 jit_solution(2750653464107480190)
XLA Ops:
  7.2 0.7 all-gather.2.cloned.1.call-update
  8.0 57.2 %all-gather.2.cloned.1.call-done = bf16[2048,1024]{1,0:T(8,128)(2,1)} async-done(((bf16[512,1024]{1,0:T(8,128)(2,1)}), bf16[2048,1024]{1,0:T(8,128)(2,1)}) %all-gather.2.cloned.1.call-update) | async-done | bytes 4194320 | tf_op jit(solution)/shard_map/all_gather | solution.py:31
  65.2 4.8 %fusion.36 = f32[2048,256]{1,0:T(8,128)} fusion(bf16[2048,1024]{1,0:T(8,128)(2,1)} %all-gather.2.cloned.1.call-done, bf16[1024,256]{1,0:T(8,128)(2,1)S(1)} %copy-done), kind=kOutput, calls=%fused_computation.78 | convolution fusion | flops 1073741824 | bytes 6815744 | tf_op jit(solution)/shard_map/dot_general | solution.py:33
  70.0 4.4 convolution_bitcast_fusion
  74.5 31.6 %reduce-scatter.8.cloned.1.call-done = f32[256,256]{1,0:T(8,128)} async-done(((f32[2048,256]{1,0:T(8,128)}), f32[256,256]{1,0:T(8,128)}) %reduce-scatter.8.cloned.1.call-update) | async-done | bytes 262160 | tf_op jit(solution)/shard_map/reduce_scatter | solution.py:32
  106.1 2.4 fusion.37
  108.8 30.9 %reduce-scatter.10.cloned.1.call-done = f32[256,4]{1,0:T(8,128)} async-done(((f32[2048,4]{1,0:T(8,128)}), f32[256,4]{1,0:T(8,128)}) %reduce-scatter.10.cloned.1.call-update) | async-done | bytes 4112
  139.7 1.0 copy.18
  140.7 54.8 %all-reduce.3.cloned.1.call-done = f32[256,256]{0,1:T(8,128)} async-done(((f32[256,256]{0,1:T(8,128)}), f32[256,256]{0,1:T(8,128)}) %all-reduce.3.cloned.1.call-update) | async-done | bytes 262160 | tf_op jit(solution)/shard_map/psum | solution.py:42
  195.5 1.1 copy.11
  196.6 1.0 fusion.11
  197.6 11.7 %cholesky.64 = f32[128,128]{1,0:T(8,128)S(1)} custom-call(f32[128,128]{1,0:T(8,128)S(1)} %cholesky.153), custom_call_target="Cholesky" | custom-call | tf_op jit(solution)/shard_map/jit(cholesky)/cholesky | solution.py:43
  209.4 9.8 %custom-call.23 = f32[1,128,128]{1,2,0:T(8,128)S(1)} custom-call(f32[1,128,128]{2,1,0:T(8,128)S(1)} %get-tuple-element.206), custom_call_target="InvertDiagBlocksLowerTriangular" | custom-call | tf_op jit(solution)/shard_map/jit(cholesky)/cholesky | solution.py:43
  219.4 0.3 convolution_subtract_fusion.3
  219.7 11.7 %cholesky.131 = f32[128,128]{1,0:T(8,128)S(1)} custom-call(f32[128,128]{1,0:T(8,128)S(1)} %convolution_subtract_fusion.3), custom_call_target="Cholesky" | custom-call | tf_op jit(solution)/shard_map/jit(cholesky)/cholesky | solution.py:43
  231.4 0.7 compare_reduce_fusion.1
  233.5 4.2 while.27
  233.7 0.7 fusion.105
  234.4 1.3 bitcast_dynamic-update-slice_fusion.4
  235.7 0.7 fusion.105
  236.4 1.3 bitcast_dynamic-update-slice_fusion.4
  237.8 19.7 %custom-call.31 = f32[2,128,128]{1,2,0:T(8,128)S(1)} custom-call(f32[2,128,128]{2,1,0:T(8,128)S(1)} %get-tuple-element.168), custom_call_target="InvertDiagBlocksLowerTriangular" | custom-call | tf_op jit(solution)/shard_map/triangular_solve/custom-call.4 | solution.py:24
  257.4 133.4 %while.26 = (s32[]{:T(128)}, f32[4,256]{1,0:T(4,128)S(1)}, f32[4,256]{1,0:T(4,128)S(1)}, s32[]{:T(128)}, f32[256,256]{1,0:T(8,128)S(1)}, /*index=5*/f32[256,256]{1,0:T(8,128)S(1)}, s32[]{:T(128)}, s32[]{:T(128)}, s32[]{:T(128)}) while((s32[]{:T(128)}, f32[4,256]{1,0:T(4,128)S(1)}, f32[4,256]{1,0:T(4,128)S(1)}, s32[]{:T(128)}, ...), condition=%wide.region_9.12_spmd.clone, body=%wide.region_7.0_spmd.clone.sunk | while | flops 11149320 | bytes 1659231 | solution.py:60
  257.6 4.1 while.28
  257.6 0.7 fusion.106
  258.3 1.3 bitcast_dynamic-update-slice_fusion.5
  259.6 0.7 fusion.106
  260.3 1.3 bitcast_dynamic-update-slice_fusion.5
  261.6 19.7 %custom-call.37 = f32[2,128,128]{1,2,0:T(8,128)S(1)} custom-call(f32[2,128,128]{2,1,0:T(8,128)S(1)} %get-tuple-element.303), custom_call_target="InvertDiagBlocksLowerTriangular" | custom-call | tf_op jit(solution)/shard_map/while/body/eval_jaxpr/triangular_solve/custom-call.4 | solution.py:24
  281.5 13.7 %psum.45 = f32[256,4]{0,1:T(4,128)S(1)} all-reduce(f32[256,4]{0,1:T(4,128)S(1)} %fusion.99), channel_id=1, replica_groups=mesh['section'=4,'row'=8] {'row'}, use_global_device_ids=true, to_apply=%region_8.8 | all-reduce | flops 1024 | bytes 8192 | tf_op jit(solution)/shard_map/while/body/eval_jaxpr/psum | solution.py:47
  296.4 0.3 fusion.104
  296.7 3.4 collective-permute-start
  300.1 1.3 collective-permute-done
  301.5 4.1 while.28
  301.5 0.7 fusion.106
  302.2 1.3 bitcast_dynamic-update-slice_fusion.5
  303.6 0.7 fusion.106
  304.2 1.3 bitcast_dynamic-update-slice_fusion.5
  305.6 19.7 %custom-call.37 = f32[2,128,128]{1,2,0:T(8,128)S(1)} custom-call(f32[2,128,128]{2,1,0:T(8,128)S(1)} %get-tuple-element.303), custom_call_target="InvertDiagBlocksLowerTriangular" | custom-call | tf_op jit(solution)/shard_map/while/body/eval_jaxpr/triangular_solve/custom-call.4 | solution.py:24
  325.5 13.6 %psum.45 = f32[256,4]{0,1:T(4,128)S(1)} all-reduce(f32[256,4]{0,1:T(4,128)S(1)} %fusion.99), channel_id=1, replica_groups=mesh['section'=4,'row'=8] {'row'}, use_global_device_ids=true, to_apply=%region_8.8 | all-reduce | flops 1024 | bytes 8192 | tf_op jit(solution)/shard_map/while/body/eval_jaxpr/psum | solution.py:47
  340.2 0.3 fusion.104
  340.6 4.2 collective-permute-start
  344.8 1.3 collective-permute-done
  346.2 4.1 while.28
  346.2 0.7 fusion.106
  346.9 1.3 bitcast_dynamic-update-slice_fusion.5
  348.2 0.7 fusion.106
  348.9 1.3 bitcast_dynamic-update-slice_fusion.5
  350.3 19.7 %custom-call.37 = f32[2,128,128]{1,2,0:T(8,128)S(1)} custom-call(f32[2,128,128]{2,1,0:T(8,128)S(1)} %get-tuple-element.303), custom_call_target="InvertDiagBlocksLowerTriangular" | custom-call | tf_op jit(solution)/shard_map/while/body/eval_jaxpr/triangular_solve/custom-call.4 | solution.py:24
  370.2 13.6 %psum.45 = f32[256,4]{0,1:T(4,128)S(1)} all-reduce(f32[256,4]{0,1:T(4,128)S(1)} %fusion.99), channel_id=1, replica_groups=mesh['section'=4,'row'=8] {'row'}, use_global_device_ids=true, to_apply=%region_8.8 | all-reduce | flops 1024 | bytes 8192 | tf_op jit(solution)/shard_map/while/body/eval_jaxpr/psum | solution.py:47
  384.9 0.3 fusion.104
  385.2 4.3 collective-permute-start
  389.6 1.3 collective-permute-done
  391.1 13.6 %psum.40 = f32[256,4]{0,1:T(4,128)S(1)} all-reduce(f32[256,4]{0,1:T(4,128)S(1)} %fusion.38), channel_id=1, replica_groups=mesh['section'=4,'row'=8] {'row'}, use_global_device_ids=true, to_apply=%region_10.13 | all-reduce | flops 1024 | bytes 8192 | tf_op jit(solution)/shard_map/psum | solution.py:47
  405.9 1.0 convolution_bitcast_fusion.1
  407.0 0.3 fusion.10
  407.2 11.0 %psum.41 = f32[4,256]{1,0:T(4,128)S(1)} all-reduce(f32[4,256]{1,0:T(4,128)S(1)} %fusion.10), channel_id=1, replica_groups=mesh['section'=4,'row'=8] {'section'}, use_global_device_ids=true, to_apply=%region_11.14 | all-reduce | flops 1024 | bytes 8192 | tf_op jit(solution)/shard_map/psum | solution.py:15
  418.3 13.6 %psum.42 = f32[4,4]{0,1:T(4,128)S(1)} all-reduce(f32[4,4]{0,1:T(4,128)S(1)} %fusion.39), channel_id=1, replica_groups=mesh['section'=4,'row'=8] {'row'}, use_global_device_ids=true, to_apply=%region_12.15 | all-reduce | flops 16 | bytes 128 | tf_op jit(solution)/shard_map/psum | solution.py:73
  432.0 0.4 cholesky.144
  432.4 0.6 compare_reduce_fusion
  433.1 0.6 fusion.25
  433.7 0.3 custom-call.24
  434.1 1.0 copy.20
  435.0 0.8 fusion.22
  (84 shorter events, 6.9 us)
Async XLA Ops:
  7.2 58.0 %copy-start = (bf16[1024,256]{1,0:T(8,128)(2,1)S(1)}, bf16[1024,256]{1,0:T(8,128)(2,1)}, u32[]{:S(2)}) copy-start(bf16[1024,256]{1,0:T(8,128)(2,1)} %param.10) | copy-start | bytes 1572868
  7.2 58.0 %all-gather.2.cloned.1.call-start = ((), (), s32[]{:S(2)}) async-start(), calls=%async_computation.3 | async-start | bytes 5242880 | tf_op jit(solution)/shard_map/all_gather | solution.py:31
  7.9 62.1 %copy-start.3 = (bf16[4,1024]{1,0:T(4,128)(2,1)S(1)}, bf16[4,1024]{1,0:T(4,128)(2,1)}, u32[]{:S(2)}) copy-start(bf16[4,1024]{1,0:T(4,128)(2,1)} %param.11) | copy-start | bytes 24580
  7.9 98.2 %reduce-scatter.8.cloned.1.call-start = ((), (), s32[]{:S(2)}) async-start(), calls=%async_computation.4 | async-start | bytes 2359296 | tf_op jit(solution)/shard_map/reduce_scatter | solution.py:32
  70.0 69.7 %reduce-scatter.10.cloned.1.call-start = ((), (), s32[]{:S(2)}) async-start(), calls=%async_computation.6 | async-start | bytes 1179648
  74.5 121.0 %all-reduce.3.cloned.1.call-start = ((), (), s32[]{:S(2)}) async-start(), calls=%async_computation.5 | async-start | bytes 524288 | tf_op jit(solution)/shard_map/psum | solution.py:42
  106.1 151.3 %copy-start.1 = (f32[256,256]{1,0:T(8,128)S(1)}, f32[256,256]{1,0:T(8,128)}, u32[]{:S(2)}) copy-start(f32[256,256]{1,0:T(8,128)} %reduce-scatter.8.cloned.1.call-done) | copy-start | bytes 786436
  108.5 325.5 %reduce-scatter.12.cloned.1.call-start = ((), (), s32[]{:S(2)}) async-start(), calls=%async_computation.7 | async-start | bytes 655360
  296.7 4.7 %collective-permute-start = (f32[4,256]{1,0:T(4,128)S(1)}, f32[4,256]{1,0:T(4,128)S(1)}, u32[]{:S(2)}, u32[]{:S(2)}) collective-permute-start(f32[4,256]{1,0:T(4,128)S(1)} %fusion.104), channel_id=1, source_target_pairs={{0,8},{8,16},{16,24},{1,9},{9,17},{17,25},{2,10},{10,18},{18,26},{... | collective-permute-start | bytes 12296 | tf_op jit(solution)/shard_map/while/body/eval_jaxpr/ppermute | solution.py:10
  340.6 5.6 %collective-permute-start = (f32[4,256]{1,0:T(4,128)S(1)}, f32[4,256]{1,0:T(4,128)S(1)}, u32[]{:S(2)}, u32[]{:S(2)}) collective-permute-start(f32[4,256]{1,0:T(4,128)S(1)} %fusion.104), channel_id=1, source_target_pairs={{0,8},{8,16},{16,24},{1,9},{9,17},{17,25},{2,10},{10,18},{18,26},{... | collective-permute-start | bytes 12296 | tf_op jit(solution)/shard_map/while/body/eval_jaxpr/ppermute | solution.py:10
  385.2 5.6 %collective-permute-start = (f32[4,256]{1,0:T(4,128)S(1)}, f32[4,256]{1,0:T(4,128)S(1)}, u32[]{:S(2)}, u32[]{:S(2)}) collective-permute-start(f32[4,256]{1,0:T(4,128)S(1)} %fusion.104), channel_id=1, source_target_pairs={{0,8},{8,16},{16,24},{1,9},{9,17},{17,25},{2,10},{10,18},{18,26},{... | collective-permute-start | bytes 12296 | tf_op jit(solution)/shard_map/while/body/eval_jaxpr/ppermute | solution.py:10
  405.9 30.0 %copy-start.2 = (f32[4,256]{1,0:T(4,128)}, f32[4,256]{1,0:T(4,128)S(1)}, u32[]{:S(2)}) copy-start(f32[4,256]{1,0:T(4,128)S(1)} %bitcast_select_fusion.1) | copy-start | bytes 12292
Sparse Core Ops, SparseCore 0:
  9.8 55.2 all-gather.1
  70.1 35.9 reduce-scatter.7
  108.4 31.2 reduce-scatter.9
  141.9 53.5 all-reduce.2
  407.1 25.7 reduce-scatter.11
where the time goes:
time: 443 us; the launch traced here: 442 us
  waiting for transfers between devices  179 us (40%)
  other arithmetic  116 us (26%)
  blocking collectives  79.1 us (18%)
  matrix products  20.6 us (5%)
  local copies, waits for them, and re-layouts  19.6 us (4%)
  between operations  15.2 us (3%)
  starting transfers between devices  12.4 us (3%)
    another operation x16, other arithmetic, factor_solve(): lax.linalg.triangular_solve(factor, half, left_side=True, lower=True, tra...  78.8 us
    all_gather x1, waiting for transfers between devices, body(): whole = lax.all_gather(omega, 'section', axis=0, tiled=True)  57.2 us
    psum x1, waiting for transfers between devices, body(): gram = lax.psum(jnp.dot(sketch.T, sketch, precision=hi), 'row')  54.8 us
    psum x4, blocking collectives, project(): inner = lax.psum(inner, 'row')  54.5 us
    another operation x6, other arithmetic, body(): factor = jnp.linalg.cholesky(gram)  34 us
    unnamed x7, waiting for transfers between devices  31.7 us
    reduce_scatter x1, waiting for transfers between devices, body(): lax.psum_scatter(jnp.dot(whole, basis, preferred_element_type=jnp.float32...  31.6 us
    another operation x28, local copies, waits for them, and re-layouts, factor_solve(): lax.linalg.triangular_solve(factor, half, left_side=True, lower=True, tra...  16.4 us
  transfers between devices with their start and end apart: 8, of which 7 were waited for; matrix products, arithmetic and copies ran while one was open for 2% of the time, Pallas kernels for 0%

commit v1 on v0

--- a/solution.py
+++ b/solution.py
@@ -25,6 +25,10 @@
 
 
 def body(omega, basis, vectors):
+
+    def list_the_body(array_here, a_name="row"):
+        return lax.all_gather(array_here, a_name).sum(axis=0)
+
     hi = lax.Precision.HIGHEST
     sections = lax.axis_size("section")
     my_section = lax.axis_index("section")
@@ -39,7 +43,7 @@
         vectors, whole, (((1,), (1,)), ((), ())), preferred_element_type=jnp.float32
     )
     probe = lax.psum_scatter(probe_term, "row", scatter_dimension=1, tiled=True)
-    gram = lax.psum(jnp.dot(sketch.T, sketch, precision=hi), "row")
+    gram = list_the_body(jnp.dot(sketch.T, sketch, precision=hi))
     factor = jnp.linalg.cholesky(gram)
 
     def project(current):

time: 443 us -> 417 us (0.941)
  waiting for transfers between devices: 179 us -> 152 us
    psum x1 -> x0, waiting for transfers between devices: 54.8 us -> none  [body(): gram = lax.psum(jnp.dot(sketch.T, sketch, precision=hi), 'row')]
    all_gather x0 -> x1, waiting for transfers between devices: none -> 27.8 us  [list_the_body(): return lax.all_gather(array_here, a_name).sum(axis=0)]
where the time goes in v1:
time: 417 us
  waiting for transfers between devices  152 us (36%)
  other arithmetic  117 us (28%)
  blocking collectives  80.7 us (19%)
  matrix products  20.7 us (5%)
  local copies, waits for them, and re-layouts  18.6 us (4%)
  between operations  15.2 us (4%)
  starting transfers between devices  12.4 us (3%)
    another operation x16, other arithmetic, factor_solve(): lax.linalg.triangular_solve(factor, half, left_side=True, lower=True, tra...  78.8 us
    all_gather x1, waiting for transfers between devices, body(): whole = lax.all_gather(omega, 'section', axis=0, tiled=True)  57.2 us
    psum x4, blocking collectives, project(): inner = lax.psum(inner, 'row')  56.1 us
    another operation x6, other arithmetic, body(): factor = jnp.linalg.cholesky(gram)  34 us
    unnamed x7, waiting for transfers between devices  31.6 us
    reduce_scatter x1, waiting for transfers between devices, body(): lax.psum_scatter(jnp.dot(whole, basis, preferred_element_type=jnp.float32...  31.6 us
    all_gather x1, waiting for transfers between devices, list_the_body(): return lax.all_gather(array_here, a_name).sum(axis=0)  27.8 us
    another operation x28, local copies, waits for them, and re-layouts, factor_solve(): lax.linalg.triangular_solve(factor, half, left_side=True, lower=True, tra...  16.4 us
  transfers between devices with their start and end apart: 8, of which 7 were waited for; matrix products, arithmetic and copies ran while one was open for 2% of the time, Pallas kernels for 0%

profile of v1, /device:TPU:0, one launch (start us, length us, event | category | flops | bytes accessed | tf_op | source)
XLA Modules:
  0.0 416.8 jit_solution(15039774899359144012)
XLA Ops:
  7.2 0.7 all-gather.4.cloned.1.call-update
  8.0 57.2 %all-gather.4.cloned.1.call-done = bf16[2048,1024]{1,0:T(8,128)(2,1)} async-done(((bf16[512,1024]{1,0:T(8,128)(2,1)}), bf16[2048,1024]{1,0:T(8,128)(2,1)}) %all-gather.4.cloned.1.call-update) | async-done | bytes 4194320 | tf_op jit(solution)/shard_map/all_gather | solution.py:35
  65.2 4.8 %fusion.36 = f32[2048,256]{1,0:T(8,128)} fusion(bf16[2048,1024]{1,0:T(8,128)(2,1)} %all-gather.4.cloned.1.call-done, bf16[1024,256]{1,0:T(8,128)(2,1)S(1)} %copy-done), kind=kOutput, calls=%fused_computation.78 | convolution fusion | flops 1073741824 | bytes 6815744 | tf_op jit(solution)/shard_map/dot_general | solution.py:37
  70.0 4.4 %convolution_bitcast_fusion = f32[2048,4]{1,0:T(8,128)} fusion(bf16[4,1024]{1,0:T(4,128)(2,1)S(1)} %copy-done.3, bf16[2048,1024]{1,0:T(8,128)(2,1)} %all-gather.4.cloned.1.call-done), kind=kOutput, calls=%fused_computation.23 | convolution fusion | flops 16777216 | bytes 4235264
  74.5 31.6 %reduce-scatter.8.cloned.1.call-done = f32[256,256]{1,0:T(8,128)} async-done(((f32[2048,256]{1,0:T(8,128)}), f32[256,256]{1,0:T(8,128)}) %reduce-scatter.8.cloned.1.call-update) | async-done | bytes 262160 | tf_op jit(solution)/shard_map/reduce_scatter | solution.py:36
  106.1 2.4 fusion.37
  108.6 0.2 reduce-scatter.12.cloned.1.call-start
  108.8 30.9 %reduce-scatter.10.cloned.1.call-done = f32[256,4]{1,0:T(8,128)} async-done(((f32[2048,4]{1,0:T(8,128)}), f32[256,4]{1,0:T(8,128)}) %reduce-scatter.10.cloned.1.call-update) | async-done | bytes 4112
  139.7 1.0 copy.15
  140.7 27.8 %all-gather.6.cloned.1.call-done = f32[2048,256]{1,0:T(8,128)} async-done(((f32[256,256]{1,0:T(8,128)}), f32[2048,256]{1,0:T(8,128)}) %all-gather.6.cloned.1.call-update) | async-done | bytes 2097168 | tf_op jit(solution)/shard_map/all_gather | solution.py:30
  168.5 1.8 reduce_sum.9
  170.5 11.7 %cholesky.64 = f32[128,128]{1,0:T(8,128)S(1)} custom-call(f32[128,128]{1,0:T(8,128)S(1)} %cholesky.153), custom_call_target="Cholesky" | custom-call | tf_op jit(solution)/shard_map/jit(cholesky)/cholesky | solution.py:47
  182.3 9.8 %custom-call.23 = f32[1,128,128]{1,2,0:T(8,128)S(1)} custom-call(f32[1,128,128]{2,1,0:T(8,128)S(1)} %get-tuple-element.206), custom_call_target="InvertDiagBlocksLowerTriangular" | custom-call | tf_op jit(solution)/shard_map/jit(cholesky)/cholesky | solution.py:47
  192.3 0.3 convolution_subtract_fusion.3
  192.5 11.7 %cholesky.131 = f32[128,128]{1,0:T(8,128)S(1)} custom-call(f32[128,128]{1,0:T(8,128)S(1)} %convolution_subtract_fusion.3), custom_call_target="Cholesky" | custom-call | tf_op jit(solution)/shard_map/jit(cholesky)/cholesky | solution.py:47
  204.3 0.7 compare_reduce_fusion.1
  206.4 4.2 %while.27 = (s32[]{:T(128)}, f32[256,256]{1,0:T(8,128)S(1)}, s32[2,2]{1,0:T(2,128)S(1)}, f32[2,128,128]{2,1,0:T(8,128)S(1)}, s32[]{:T(128)}) while((s32[]{:T(128)}, f32[256,256]{1,0:T(8,128)S(1)}, s32[2,2]{1,0:T(2,128)S(1)}, f32[2,128,128]{2,1,0:T(8,128)S(1)}, s32[]{:T(128)}) %tuple.89), condition=%wide.while_cond.1.clone, body=%wide.while_body.1.clone.sunk | while | flops 2 | bytes 131189 | solution.py:24
  206.6 0.7 fusion.105
  207.2 1.3 bitcast_dynamic-update-slice_fusion.4
  208.6 0.7 fusion.105
  209.3 1.3 bitcast_dynamic-update-slice_fusion.4
  210.6 19.7 %custom-call.31 = f32[2,128,128]{1,2,0:T(8,128)S(1)} custom-call(f32[2,128,128]{2,1,0:T(8,128)S(1)} %get-tuple-element.168), custom_call_target="InvertDiagBlocksLowerTriangular" | custom-call | tf_op jit(solution)/shard_map/triangular_solve/custom-call.4 | solution.py:24
  230.3 135.0 %while.26 = (s32[]{:T(128)}, f32[4,256]{1,0:T(4,128)S(1)}, f32[4,256]{1,0:T(4,128)S(1)}, s32[]{:T(128)}, f32[256,256]{1,0:T(8,128)S(1)}, /*index=5*/f32[256,256]{1,0:T(8,128)S(1)}, s32[]{:T(128)}, s32[]{:T(128)}, s32[]{:T(128)}) while((s32[]{:T(128)}, f32[4,256]{1,0:T(4,128)S(1)}, f32[4,256]{1,0:T(4,128)S(1)}, s32[]{:T(128)}, ...), condition=%wide.region_9.12_spmd.clone, body=%wide.region_7.0_spmd.clone.sunk | while | flops 11149320 | bytes 1659231 | solution.py:64
  230.5 4.1 while.28
  230.5 0.7 fusion.106
  231.1 1.3 bitcast_dynamic-update-slice_fusion.5
  232.5 0.7 fusion.106
  233.2 1.3 bitcast_dynamic-update-slice_fusion.5
  234.5 19.7 %custom-call.37 = f32[2,128,128]{1,2,0:T(8,128)S(1)} custom-call(f32[2,128,128]{2,1,0:T(8,128)S(1)} %get-tuple-element.303), custom_call_target="InvertDiagBlocksLowerTriangular" | custom-call | tf_op jit(solution)/shard_map/while/body/eval_jaxpr/triangular_solve/custom-call.4 | solution.py:24
  254.4 15.3 %psum.37 = f32[256,4]{0,1:T(4,128)S(1)} all-reduce(f32[256,4]{0,1:T(4,128)S(1)} %fusion.99), channel_id=1, replica_groups=mesh['section'=4,'row'=8] {'row'}, use_global_device_ids=true, to_apply=%region_8.8 | all-reduce | flops 1024 | bytes 8192 | tf_op jit(solution)/shard_map/while/body/eval_jaxpr/psum | solution.py:51
  270.8 0.3 fusion.104
  271.2 3.4 collective-permute-start
  274.6 1.3 collective-permute-done
  276.0 4.1 while.28
  276.0 0.7 fusion.106
  276.7 1.3 bitcast_dynamic-update-slice_fusion.5
  278.0 0.7 fusion.106
  278.7 1.3 bitcast_dynamic-update-slice_fusion.5
  280.1 19.7 %custom-call.37 = f32[2,128,128]{1,2,0:T(8,128)S(1)} custom-call(f32[2,128,128]{2,1,0:T(8,128)S(1)} %get-tuple-element.303), custom_call_target="InvertDiagBlocksLowerTriangular" | custom-call | tf_op jit(solution)/shard_map/while/body/eval_jaxpr/triangular_solve/custom-call.4 | solution.py:24
  300.0 13.6 %psum.37 = f32[256,4]{0,1:T(4,128)S(1)} all-reduce(f32[256,4]{0,1:T(4,128)S(1)} %fusion.99), channel_id=1, replica_groups=mesh['section'=4,'row'=8] {'row'}, use_global_device_ids=true, to_apply=%region_8.8 | all-reduce | flops 1024 | bytes 8192 | tf_op jit(solution)/shard_map/while/body/eval_jaxpr/psum | solution.py:51
  314.7 0.3 fusion.104
  315.0 4.2 %collective-permute-start = (f32[4,256]{1,0:T(4,128)S(1)}, f32[4,256]{1,0:T(4,128)S(1)}, u32[]{:S(2)}, u32[]{:S(2)}) collective-permute-start(f32[4,256]{1,0:T(4,128)S(1)} %fusion.104), channel_id=1, source_target_pairs={{0,8},{8,16},{16,24},{1,9},{9,17},{17,25},{2,10},{10,18},{18,26},{... | collective-permute-start | bytes 12296 | tf_op jit(solution)/shard_map/while/body/eval_jaxpr/ppermute | solution.py:10
  319.3 1.3 collective-permute-done
  320.7 4.1 while.28
  320.7 0.7 fusion.106
  321.3 1.3 bitcast_dynamic-update-slice_fusion.5
  322.7 0.7 fusion.106
  323.4 1.3 bitcast_dynamic-update-slice_fusion.5
  324.7 19.7 %custom-call.37 = f32[2,128,128]{1,2,0:T(8,128)S(1)} custom-call(f32[2,128,128]{2,1,0:T(8,128)S(1)} %get-tuple-element.303), custom_call_target="InvertDiagBlocksLowerTriangular" | custom-call | tf_op jit(solution)/shard_map/while/body/eval_jaxpr/triangular_solve/custom-call.4 | solution.py:24
  344.6 13.6 %psum.37 = f32[256,4]{0,1:T(4,128)S(1)} all-reduce(f32[256,4]{0,1:T(4,128)S(1)} %fusion.99), channel_id=1, replica_groups=mesh['section'=4,'row'=8] {'row'}, use_global_device_ids=true, to_apply=%region_8.8 | all-reduce | flops 1024 | bytes 8192 | tf_op jit(solution)/shard_map/while/body/eval_jaxpr/psum | solution.py:51
  359.4 0.3 fusion.104
  359.7 4.3 %collective-permute-start = (f32[4,256]{1,0:T(4,128)S(1)}, f32[4,256]{1,0:T(4,128)S(1)}, u32[]{:S(2)}, u32[]{:S(2)}) collective-permute-start(f32[4,256]{1,0:T(4,128)S(1)} %fusion.104), channel_id=1, source_target_pairs={{0,8},{8,16},{16,24},{1,9},{9,17},{17,25},{2,10},{10,18},{18,26},{... | collective-permute-start | bytes 12296 | tf_op jit(solution)/shard_map/while/body/eval_jaxpr/ppermute | solution.py:10
  364.0 1.3 collective-permute-done
  365.5 13.6 %psum.32 = f32[256,4]{0,1:T(4,128)S(1)} all-reduce(f32[256,4]{0,1:T(4,128)S(1)} %fusion.38), channel_id=1, replica_groups=mesh['section'=4,'row'=8] {'row'}, use_global_device_ids=true, to_apply=%region_10.13 | all-reduce | flops 1024 | bytes 8192 | tf_op jit(solution)/shard_map/psum | solution.py:51
  380.4 1.1 convolution_bitcast_fusion.1
  381.4 0.3 fusion.10
  381.7 10.9 %psum.33 = f32[4,256]{1,0:T(4,128)S(1)} all-reduce(f32[4,256]{1,0:T(4,128)S(1)} %fusion.10), channel_id=1, replica_groups=mesh['section'=4,'row'=8] {'section'}, use_global_device_ids=true, to_apply=%region_11.14 | all-reduce | flops 1024 | bytes 8192 | tf_op jit(solution)/shard_map/psum | solution.py:15
  392.8 13.6 %psum.34 = f32[4,4]{0,1:T(4,128)S(1)} all-reduce(f32[4,4]{0,1:T(4,128)S(1)} %fusion.39), channel_id=1, replica_groups=mesh['section'=4,'row'=8] {'row'}, use_global_device_ids=true, to_apply=%region_12.15 | all-reduce | flops 16 | bytes 128 | tf_op jit(solution)/shard_map/psum | solution.py:77
  406.5 0.4 cholesky.144
  406.9 0.6 compare_reduce_fusion
  407.5 0.6 fusion.25
  408.2 0.3 custom-call.24
  408.5 1.0 copy.17
  409.5 0.8 fusion.22
  (85 shorter events, 6.9 us)
Async XLA Ops:
  7.2 58.0 %copy-start = (bf16[1024,256]{1,0:T(8,128)(2,1)S(1)}, bf16[1024,256]{1,0:T(8,128)(2,1)}, u32[]{:S(2)}) copy-start(bf16[1024,256]{1,0:T(8,128)(2,1)} %param.10) | copy-start | bytes 1572868
  7.2 58.0 %all-gather.4.cloned.1.call-start = ((), (), s32[]{:S(2)}) async-start(), calls=%async_computation.3 | async-start | bytes 5242880 | tf_op jit(solution)/shard_map/all_gather | solution.py:35
  7.9 62.1 %copy-start.3 = (bf16[4,1024]{1,0:T(4,128)(2,1)S(1)}, bf16[4,1024]{1,0:T(4,128)(2,1)}, u32[]{:S(2)}) copy-start(bf16[4,1024]{1,0:T(4,128)(2,1)} %param.11) | copy-start | bytes 24580
  7.9 98.2 %reduce-scatter.8.cloned.1.call-start = ((), (), s32[]{:S(2)}) async-start(), calls=%async_computation.4 | async-start | bytes 2359296 | tf_op jit(solution)/shard_map/reduce_scatter | solution.py:36
  70.0 69.7 %reduce-scatter.10.cloned.1.call-start = ((), (), s32[]{:S(2)}) async-start(), calls=%async_computation.6 | async-start | bytes 1179648
  74.5 94.1 %all-gather.6.cloned.1.call-start = ((), (), s32[]{:S(2)}) async-start(), calls=%async_computation.5 | async-start | bytes 2359296 | tf_op jit(solution)/shard_map/all_gather | solution.py:30
  106.1 124.2 %copy-start.1 = (f32[256,256]{1,0:T(8,128)S(1)}, f32[256,256]{1,0:T(8,128)}, u32[]{:S(2)}) copy-start(f32[256,256]{1,0:T(8,128)} %reduce-scatter.8.cloned.1.call-done) | copy-start | bytes 786436
  108.6 300.0 %reduce-scatter.12.cloned.1.call-start = ((), (), s32[]{:S(2)}) async-start(), calls=%async_computation.7 | async-start | bytes 655360
  271.2 4.7 %collective-permute-start = (f32[4,256]{1,0:T(4,128)S(1)}, f32[4,256]{1,0:T(4,128)S(1)}, u32[]{:S(2)}, u32[]{:S(2)}) collective-permute-start(f32[4,256]{1,0:T(4,128)S(1)} %fusion.104), channel_id=1, source_target_pairs={{0,8},{8,16},{16,24},{1,9},{9,17},{17,25},{2,10},{10,18},{18,26},{... | collective-permute-start | bytes 12296 | tf_op jit(solution)/shard_map/while/body/eval_jaxpr/ppermute | solution.py:10
  315.0 5.6 %collective-permute-start = (f32[4,256]{1,0:T(4,128)S(1)}, f32[4,256]{1,0:T(4,128)S(1)}, u32[]{:S(2)}, u32[]{:S(2)}) collective-permute-start(f32[4,256]{1,0:T(4,128)S(1)} %fusion.104), channel_id=1, source_target_pairs={{0,8},{8,16},{16,24},{1,9},{9,17},{17,25},{2,10},{10,18},{18,26},{... | collective-permute-start | bytes 12296 | tf_op jit(solution)/shard_map/while/body/eval_jaxpr/ppermute | solution.py:10
  359.7 5.6 %collective-permute-start = (f32[4,256]{1,0:T(4,128)S(1)}, f32[4,256]{1,0:T(4,128)S(1)}, u32[]{:S(2)}, u32[]{:S(2)}) collective-permute-start(f32[4,256]{1,0:T(4,128)S(1)} %fusion.104), channel_id=1, source_target_pairs={{0,8},{8,16},{16,24},{1,9},{9,17},{17,25},{2,10},{10,18},{18,26},{... | collective-permute-start | bytes 12296 | tf_op jit(solution)/shard_map/while/body/eval_jaxpr/ppermute | solution.py:10
  380.3 30.0 %copy-start.2 = (f32[4,256]{1,0:T(4,128)}, f32[4,256]{1,0:T(4,128)S(1)}, u32[]{:S(2)}) copy-start(f32[4,256]{1,0:T(4,128)S(1)} %bitcast_select_fusion.1) | copy-start | bytes 12292
Sparse Core Ops, SparseCore 0:
  9.8 55.2 all-gather.3
  70.1 35.9 reduce-scatter.7
  108.4 31.2 reduce-scatter.9
  141.2 27.3 all-gather.5
  381.6 25.7 reduce-scatter.11
